TPU v7x, 32 devices: a whole 2x2x4 slice. The times are simulated.
32 devices in a mesh: patch: 8 (over z, y), dir: 4 (over x, core).
Axes of the slice: x: 2, y: 2, z: 4, core: 2. Of those that a mesh axis runs over, the one named last changes fastest.
Arguments:
- right_side: float32 [96, 192, 256], P('dir', 'patch'), may hold values from -6 to 6
- guess: float32 [96, 192, 256], P('dir', 'patch'), may hold values from -3 to 3
- mask_fine: int32 [96, 192, 2], P('dir', 'patch'), may hold values 0 or 1
- mask_next: int32 [48, 96, 1], P('dir', 'patch'), may hold values 0 or 1
Outputs:
- solution: float32 [96, 192, 256], P('dir', 'patch')
All inputs are finite; a program needn't handle non-finite values. No bound on the sum of `mask_fine` or of `mask_next` on one device may be relied on, other than what follows from the above.
Results may differ from a plain program's by a relative error of at most 0.00005.
Values sent between devices are 32-bit elements; how exact they have to be, the bound alone decides.
A program may use at most 64 MiB of HBM per device.

v0:
```python
import jax
import jax.numpy as jnp
from jax import lax
from jax.sharding import PartitionSpec as P

TILE = 128
SWEEPS = 3
LEVELS = 4


MASS = (
    1.0 / 5040,
    120.0 / 5040,
    1191.0 / 5040,
    2416.0 / 5040,
    1191.0 / 5040,
    120.0 / 5040,
    1.0 / 5040,
)
STIFF = (-1.0 / 120, -0.2, -0.125, 2.0 / 3, -0.125, -0.2, -1.0 / 120)
SUBDIV = (0.125, 0.5, 0.75, 0.5, 0.125)
OMEGA = 0.5
HIGHEST = lax.Precision.HIGHEST


def padded(value, sides, width):
    for axis, dim in sides:
        devices, length = (lax.axis_size(axis), value.shape[dim])
        up = [(i, (i + 1) % devices) for i in range(devices)]
        down = [(j, i) for i, j in up]
        last = lax.slice_in_dim(value, length - width, length, axis=dim)
        leading = lax.slice_in_dim(value, 0, width, axis=dim)
        before = lax.ppermute(last, axis, up)
        after = lax.ppermute(leading, axis, down)
        value = jnp.concatenate([before, value, after], axis=dim)
    return value


def table(row_count, column_count, coeffs, row_step, column_step, offset):
    row_index = lax.broadcasted_iota(jnp.int32, (row_count, column_count), 0)
    column_index = lax.broadcasted_iota(jnp.int32, (row_count, column_count), 1)
    where_at = row_step * row_index + column_step * column_index + offset
    matrix = jnp.zeros((row_count, column_count), jnp.float32)
    for position, weight_value in enumerate(coeffs):
        matrix = matrix + jnp.where(where_at == position, weight_value, 0.0).astype(jnp.float32)
    return matrix


def along_last(values, matrix):
    return jnp.einsum("uvw,jw->uvj", values, matrix, precision=HIGHEST)


def along_middle(values, matrix):
    return jnp.einsum("ij,ujw->uiw", matrix, values, precision=HIGHEST)


def along_first(values, matrix):
    old_shape = values.shape
    flat = jnp.dot(
        matrix, values.reshape(old_shape[0], old_shape[1] * old_shape[2]), precision=HIGHEST
    )
    return flat.reshape(matrix.shape[0], old_shape[1], old_shape[2])


def clear_ends(extended, width):
    position = lax.axis_index("dir")
    last_index = lax.axis_size("dir") - 1
    extent_u = extended.shape[0]
    layer_index = lax.broadcasted_iota(jnp.int32, (extent_u, 1, 1), 0)
    lower_rim = jnp.logical_and(position == 0, layer_index < width)
    upper_rim = jnp.logical_and(position == last_index, layer_index >= extent_u - width)
    return jnp.where(jnp.logical_or(lower_rim, upper_rim), 0.0, extended)


def local_tables(extent_u, extent_v, extent_w):
    return (
        table(extent_w, extent_w, MASS, -1, 1, 3),
        table(extent_w, extent_w, STIFF, -1, 1, 3),
        table(extent_v, extent_v + 6, MASS, -1, 1, 0),
        table(extent_v, extent_v + 6, STIFF, -1, 1, 0),
        table(extent_u, extent_u + 6, MASS, -1, 1, 0),
        table(extent_u, extent_u + 6, STIFF, -1, 1, 0),
    )


def operate(current, scale_factor, tables):
    mass_w, stiff_w, mass_v, stiff_v, mass_u, stiff_u = tables
    extended = clear_ends(padded(current, (("patch", 1), ("dir", 0)), 3), 3)
    mass_side = along_last(extended, mass_w)
    stiff_side = along_last(extended, stiff_w)
    first_term = along_middle(mass_side, mass_v)
    second = along_middle(mass_side, stiff_v) + along_middle(stiff_side, mass_v)
    return scale_factor * (along_first(first_term, stiff_u) + along_first(second, mass_u))


def smooth(current, load, scale_factor, active, tables):
    update = OMEGA / scale_factor * (load - operate(current, scale_factor, tables))
    if active is not None:
        update = update * active
    return current + update


def cycle(load, current, level_index, actives):
    scale_factor = float(2**level_index)
    active = actives[level_index]
    extent_u, extent_v, extent_w = load.shape
    last_level = level_index == LEVELS - 1
    tables = local_tables(extent_u, extent_v, extent_w)
    for sweep_index in range(SWEEPS):
        current = smooth(current, load, scale_factor, active, tables)
    if not last_level:
        residual_field = load - operate(current, scale_factor, tables)
        if active is not None:
            residual_field = residual_field * active
        narrowed = along_last(residual_field, table(extent_w // 2, extent_w, SUBDIV, -2, 1, 2))
        widened = clear_ends(padded(narrowed, (("patch", 1), ("dir", 0)), 2), 2)
        coarse_load = along_first(
            along_middle(widened, table(extent_v // 2, extent_v + 4, SUBDIV, -2, 1, 0)),
            table(extent_u // 2, extent_u + 4, SUBDIV, -2, 1, 0),
        )
        correction = cycle(coarse_load, jnp.zeros_like(coarse_load), level_index + 1, actives)
        spread_out = clear_ends(padded(correction, (("patch", 1), ("dir", 0)), 1), 1)
        finer = along_last(spread_out, table(extent_w, extent_w // 2, SUBDIV, 1, -2, 2))
        finer = along_middle(finer, table(extent_v, extent_v // 2 + 2, SUBDIV, 1, -2, 4))
        finer = along_first(finer, table(extent_u, extent_u // 2 + 2, SUBDIV, 1, -2, 4))
        if active is not None:
            finer = finer * active
        current = current + finer
    for sweep_index in range(SWEEPS):
        current = smooth(current, load, scale_factor, active, tables)
    return current


def on_device(right_side, guess, mask_fine, mask_next):
    actives = [
        jnp.repeat(mask_fine.astype(jnp.float32), TILE, axis=2),
        jnp.repeat(mask_next.astype(jnp.float32), TILE, axis=2),
    ] + [None] * (LEVELS - 2)
    return cycle(right_side, guess * actives[0], 0, actives)


def solution(mesh):
    in_specs = (
        P("dir", "patch", None),
        P("dir", "patch", None),
        P("dir", "patch", None),
        P("dir", "patch", None),
    )
    out_specs = P("dir", "patch", None)
    return jax.shard_map(
        on_device, mesh=mesh, in_specs=in_specs, out_specs=out_specs, check_vma=False
    )
```

profile of v0, /device:TPU:0, one launch (start us, length us, event | category | flops | bytes accessed | tf_op | source)
XLA Modules:
  0.0 450.3 jit_solution(13128966278902689817)
XLA Ops:
  0.0 6.0 %collective-permute-start.61 = (f32[3,3,32]{2,0,1:T(4,128)S(1)}, f32[3,3,32]{2,0,1:T(4,128)S(1)}, u32[]{:S(2)}, u32[]{:S(2)}) collective-permute-start(f32[3,3,32]{2,0,1:T(4,128)S(1)} %broadcast_in_dim.1139), channel_id=1, source_target_pairs={{4,0},{8,4},{12,8},{16,12},{20,16},{24,20},{28,24},{0,28},{5,1},{9... | collective-permute-start | bytes 3464 | tf_op jit(solution)/shard_map/ppermute | solution.py:34
  6.0 4.7 %collective-permute-start.41 = (f32[6,3,64]{2,0,1:T(8,128)S(1)}, f32[6,3,64]{2,0,1:T(8,128)S(1)}, u32[]{:S(2)}, u32[]{:S(2)}) collective-permute-start(f32[6,3,64]{2,0,1:T(8,128)S(1)} %broadcast.740), channel_id=1, source_target_pairs={{4,0},{8,4},{12,8},{16,12},{20,16},{24,20},{28,24},{0,28},{5,1},{9... | collective-permute-start | bytes 13832 | tf_op jit(solution)/shard_map/ppermute | solution.py:34
  13.9 4.7 %collective-permute-start.1 = (f32[24,3,256]{2,0,1:T(8,128)S(1)}, f32[24,3,256]{2,0,1:T(8,128)S(1)}, u32[]{:S(2)}, u32[]{:S(2)}) collective-permute-start(f32[24,3,256]{2,0,1:T(8,128)S(1)} %get-tuple-element.32), channel_id=1, source_target_pairs={{4,0},{8,4},{12,8},{16,12},{20,16},{24,20},{28,24},{0,28},{5,1},{9... | collective-permute-start | bytes 221192 | tf_op jit(solution)/shard_map/ppermute | solution.py:34
  20.9 4.7 %collective-permute-start.21 = (f32[12,3,128]{2,0,1:T(8,128)S(1)}, f32[12,3,128]{2,0,1:T(8,128)S(1)}, u32[]{:S(2)}, u32[]{:S(2)}) collective-permute-start(f32[12,3,128]{2,0,1:T(8,128)S(1)} %broadcast.703), channel_id=1, source_target_pairs={{4,0},{8,4},{12,8},{16,12},{20,16},{24,20},{28,24},{0,28},{5,1},{9... | collective-permute-start | bytes 55304 | tf_op jit(solution)/shard_map/ppermute | solution.py:34
  61.0 4.7 %collective-permute-start.9 = (f32[24,3,256]{2,0,1:T(8,128)S(1)}, f32[24,3,256]{2,0,1:T(8,128)S(1)}, u32[]{:S(2)}, u32[]{:S(2)}) collective-permute-start(f32[24,3,256]{2,0,1:T(8,128)S(1)} %get-tuple-element.28), channel_id=1, source_target_pairs={{4,0},{8,4},{12,8},{16,12},{20,16},{24,20},{28,24},{0,28},{5,1},{9... | collective-permute-start | bytes 221192 | tf_op jit(solution)/shard_map/ppermute | solution.py:34
  114.6 4.8 %collective-permute-start.25 = (f32[12,3,128]{2,0,1:T(8,128)S(1)}, f32[12,3,128]{2,0,1:T(8,128)S(1)}, u32[]{:S(2)}, u32[]{:S(2)}) collective-permute-start(f32[12,3,128]{2,0,1:T(8,128)S(1)} %get-tuple-element.70), channel_id=1, source_target_pairs={{4,0},{8,4},{12,8},{16,12},{20,16},{24,20},{28,24},{0,28},{5,1},{9... | collective-permute-start | bytes 55304 | tf_op jit(solution)/shard_map/ppermute | solution.py:34
  128.5 4.7 %collective-permute-start.29 = (f32[12,3,128]{2,0,1:T(8,128)S(1)}, f32[12,3,128]{2,0,1:T(8,128)S(1)}, u32[]{:S(2)}, u32[]{:S(2)}) collective-permute-start(f32[12,3,128]{2,0,1:T(8,128)S(1)} %get-tuple-element.68), channel_id=1, source_target_pairs={{4,0},{8,4},{12,8},{16,12},{20,16},{24,20},{28,24},{0,28},{5,1},{9... | collective-permute-start | bytes 55304 | tf_op jit(solution)/shard_map/ppermute | solution.py:34
  141.5 4.8 %collective-permute-start.33 = (f32[12,3,128]{2,0,1:T(8,128)S(1)}, f32[12,3,128]{2,0,1:T(8,128)S(1)}, u32[]{:S(2)}, u32[]{:S(2)}) collective-permute-start(f32[12,3,128]{2,0,1:T(8,128)S(1)} %get-tuple-element.66), channel_id=1, source_target_pairs={{4,0},{8,4},{12,8},{16,12},{20,16},{24,20},{28,24},{0,28},{5,1},{9... | collective-permute-start | bytes 55304 | tf_op jit(solution)/shard_map/ppermute | solution.py:34
  154.8 4.8 %collective-permute-start.37 = (f32[12,2,64]{2,1,0:T(2,128)S(1)}, f32[12,2,64]{2,1,0:T(2,128)S(1)}, u32[]{:S(2)}, u32[]{:S(2)}) collective-permute-start(f32[12,2,64]{2,1,0:T(2,128)S(1)} %get-tuple-element.64), channel_id=1, source_target_pairs={{4,0},{8,4},{12,8},{16,12},{20,16},{24,20},{28,24},{0,28},{5,1},{9... | collective-permute-start | bytes 18440 | tf_op jit(solution)/shard_map/ppermute | solution.py:34
  165.4 4.8 %collective-permute-start.45 = (f32[6,3,64]{2,0,1:T(8,128)S(1)}, f32[6,3,64]{2,0,1:T(8,128)S(1)}, u32[]{:S(2)}, u32[]{:S(2)}) collective-permute-start(f32[6,3,64]{2,0,1:T(8,128)S(1)} %get-tuple-element.104), channel_id=1, source_target_pairs={{4,0},{8,4},{12,8},{16,12},{20,16},{24,20},{28,24},{0,28},{5,1},{9... | collective-permute-start | bytes 13832 | tf_op jit(solution)/shard_map/ppermute | solution.py:34
  177.6 4.8 %collective-permute-start.49 = (f32[6,3,64]{2,0,1:T(8,128)S(1)}, f32[6,3,64]{2,0,1:T(8,128)S(1)}, u32[]{:S(2)}, u32[]{:S(2)}) collective-permute-start(f32[6,3,64]{2,0,1:T(8,128)S(1)} %get-tuple-element.102), channel_id=1, source_target_pairs={{4,0},{8,4},{12,8},{16,12},{20,16},{24,20},{28,24},{0,28},{5,1},{9... | collective-permute-start | bytes 13832 | tf_op jit(solution)/shard_map/ppermute | solution.py:34
  189.7 5.0 %collective-permute-start.53 = (f32[6,3,64]{2,0,1:T(8,128)S(1)}, f32[6,3,64]{2,0,1:T(8,128)S(1)}, u32[]{:S(2)}, u32[]{:S(2)}) collective-permute-start(f32[6,3,64]{2,0,1:T(8,128)S(1)} %get-tuple-element.100), channel_id=1, source_target_pairs={{4,0},{8,4},{12,8},{16,12},{20,16},{24,20},{28,24},{0,28},{5,1},{9... | collective-permute-start | bytes 13832 | tf_op jit(solution)/shard_map/ppermute | solution.py:34
  202.1 5.0 %collective-permute-start.57 = (f32[6,2,32]{2,1,0:T(2,128)S(1)}, f32[6,2,32]{2,1,0:T(2,128)S(1)}, u32[]{:S(2)}, u32[]{:S(2)}) collective-permute-start(f32[6,2,32]{2,1,0:T(2,128)S(1)} %get-tuple-element.98), channel_id=1, source_target_pairs={{4,0},{8,4},{12,8},{16,12},{20,16},{24,20},{28,24},{0,28},{5,1},{9... | collective-permute-start | bytes 4616 | tf_op jit(solution)/shard_map/ppermute | solution.py:34
  212.8 4.8 %collective-permute-start.65 = (f32[3,3,32]{2,0,1:T(4,128)S(1)}, f32[3,3,32]{2,0,1:T(4,128)S(1)}, u32[]{:S(2)}, u32[]{:S(2)}) collective-permute-start(f32[3,3,32]{2,0,1:T(4,128)S(1)} %fusion.128), channel_id=1, source_target_pairs={{4,0},{8,4},{12,8},{16,12},{20,16},{24,20},{28,24},{0,28},{5,1},{9... | collective-permute-start | bytes 3464 | tf_op jit(solution)/shard_map/ppermute | solution.py:34
  219.0 5.0 %collective-permute-done.64 = f32[3,3,32]{2,0,1:T(4,128)S(1)} collective-permute-done((f32[3,3,32]{2,0,1:T(4,128)S(1)}, f32[3,3,32]{2,0,1:T(4,128)S(1)}, u32[]{:S(2)}, u32[]{:S(2)}) %collective-permute-start.64) | collective-permute-done | bytes 1184 | tf_op jit(solution)/shard_map/ppermute | solution.py:33
  277.6 4.7 %collective-permute-start.85 = (f32[3,1,32]{2,0,1:T(4,128)S(1)}, f32[3,1,32]{2,0,1:T(4,128)S(1)}, u32[]{:S(2)}, u32[]{:S(2)}) collective-permute-start(f32[3,1,32]{2,0,1:T(4,128)S(1)} %get-tuple-element.108), channel_id=1, source_target_pairs={{4,0},{8,4},{12,8},{16,12},{20,16},{24,20},{28,24},{0,28},{5,1},{9... | collective-permute-start | bytes 1160 | tf_op jit(solution)/shard_map/ppermute | solution.py:34
  287.9 4.8 %collective-permute-start.89 = (f32[6,3,64]{2,0,1:T(8,128)S(1)}, f32[6,3,64]{2,0,1:T(8,128)S(1)}, u32[]{:S(2)}, u32[]{:S(2)}) collective-permute-start(f32[6,3,64]{2,0,1:T(8,128)S(1)} %get-tuple-element.96), channel_id=1, source_target_pairs={{4,0},{8,4},{12,8},{16,12},{20,16},{24,20},{28,24},{0,28},{5,1},{9... | collective-permute-start | bytes 13832 | tf_op jit(solution)/shard_map/ppermute | solution.py:34
  300.0 4.8 %collective-permute-start.93 = (f32[6,3,64]{2,0,1:T(8,128)S(1)}, f32[6,3,64]{2,0,1:T(8,128)S(1)}, u32[]{:S(2)}, u32[]{:S(2)}) collective-permute-start(f32[6,3,64]{2,0,1:T(8,128)S(1)} %get-tuple-element.94), channel_id=1, source_target_pairs={{4,0},{8,4},{12,8},{16,12},{20,16},{24,20},{28,24},{0,28},{5,1},{9... | collective-permute-start | bytes 13832 | tf_op jit(solution)/shard_map/ppermute | solution.py:34
  312.2 4.8 %collective-permute-start.97 = (f32[6,3,64]{2,0,1:T(8,128)S(1)}, f32[6,3,64]{2,0,1:T(8,128)S(1)}, u32[]{:S(2)}, u32[]{:S(2)}) collective-permute-start(f32[6,3,64]{2,0,1:T(8,128)S(1)} %get-tuple-element.92), channel_id=1, source_target_pairs={{4,0},{8,4},{12,8},{16,12},{20,16},{24,20},{28,24},{0,28},{5,1},{9... | collective-permute-start | bytes 13832 | tf_op jit(solution)/shard_map/ppermute | solution.py:34
  324.7 4.8 %collective-permute-start.101 = (f32[6,1,64]{2,0,1:T(8,128)S(1)}, f32[6,1,64]{2,0,1:T(8,128)S(1)}, u32[]{:S(2)}, u32[]{:S(2)}) collective-permute-start(f32[6,1,64]{2,0,1:T(8,128)S(1)} %get-tuple-element.90), channel_id=1, source_target_pairs={{4,0},{8,4},{12,8},{16,12},{20,16},{24,20},{28,24},{0,28},{5,1},{9... | collective-permute-start | bytes 4616 | tf_op jit(solution)/shard_map/ppermute | solution.py:34
  335.3 4.8 %collective-permute-start.105 = (f32[12,3,128]{2,0,1:T(8,128)S(1)}, f32[12,3,128]{2,0,1:T(8,128)S(1)}, u32[]{:S(2)}, u32[]{:S(2)}) collective-permute-start(f32[12,3,128]{2,0,1:T(8,128)S(1)} %get-tuple-element.62), channel_id=1, source_target_pairs={{4,0},{8,4},{12,8},{16,12},{20,16},{24,20},{28,24},{0,28},{5,1},{9... | collective-permute-start | bytes 55304 | tf_op jit(solution)/shard_map/ppermute | solution.py:34
  348.5 4.8 %collective-permute-start.109 = (f32[12,3,128]{2,0,1:T(8,128)S(1)}, f32[12,3,128]{2,0,1:T(8,128)S(1)}, u32[]{:S(2)}, u32[]{:S(2)}) collective-permute-start(f32[12,3,128]{2,0,1:T(8,128)S(1)} %get-tuple-element.60), channel_id=1, source_target_pairs={{4,0},{8,4},{12,8},{16,12},{20,16},{24,20},{28,24},{0,28},{5,1},{9... | collective-permute-start | bytes 55304 | tf_op jit(solution)/shard_map/ppermute | solution.py:34
  374.7 4.7 %collective-permute-start.117 = (f32[12,1,128]{2,0,1:T(8,128)S(1)}, f32[12,1,128]{2,0,1:T(8,128)S(1)}, u32[]{:S(2)}, u32[]{:S(2)}) collective-permute-start(f32[12,1,128]{2,0,1:T(8,128)S(1)} %get-tuple-element.56), channel_id=1, source_target_pairs={{4,0},{8,4},{12,8},{16,12},{20,16},{24,20},{28,24},{0,28},{5,1},{9... | collective-permute-start | bytes 18440 | tf_op jit(solution)/shard_map/ppermute | solution.py:34
  386.1 4.8 %collective-permute-start.121 = (f32[24,3,256]{2,0,1:T(8,128)S(1)}, f32[24,3,256]{2,0,1:T(8,128)S(1)}, u32[]{:S(2)}, u32[]{:S(2)}) collective-permute-start(f32[24,3,256]{2,0,1:T(8,128)S(1)} %get-tuple-element.24), channel_id=1, source_target_pairs={{4,0},{8,4},{12,8},{16,12},{20,16},{24,20},{28,24},{0,28},{5,1},{9... | collective-permute-start | bytes 221192 | tf_op jit(solution)/shard_map/ppermute | solution.py:34
  (708 shorter events, 330.3 us)
Async XLA Ops:
  0.0 170.2 %collective-permute-start.61 = (f32[3,3,32]{2,0,1:T(4,128)S(1)}, f32[3,3,32]{2,0,1:T(4,128)S(1)}, u32[]{:S(2)}, u32[]{:S(2)}) collective-permute-start(f32[3,3,32]{2,0,1:T(4,128)S(1)} %broadcast_in_dim.1139), channel_id=1, source_target_pairs={{4,0},{8,4},{12,8},{16,12},{20,16},{24,20},{28,24},{0,28},{5,1},{9... | collective-permute-start | bytes 3464 | tf_op jit(solution)/shard_map/ppermute | solution.py:34
  6.0 164.2 %collective-permute-start.60 = (f32[3,3,32]{2,0,1:T(4,128)S(1)}, f32[3,3,32]{2,0,1:T(4,128)S(1)}, u32[]{:S(2)}, u32[]{:S(2)}) collective-permute-start(f32[3,3,32]{2,0,1:T(4,128)S(1)} %broadcast_in_dim.1139), channel_id=1, source_target_pairs={{0,4},{4,8},{8,12},{12,16},{16,20},{20,24},{24,28},{28,0},{1,5},{5... | collective-permute-start | bytes 3464 | tf_op jit(solution)/shard_map/ppermute | solution.py:33
  6.0 19.7 %collective-permute-start.41 = (f32[6,3,64]{2,0,1:T(8,128)S(1)}, f32[6,3,64]{2,0,1:T(8,128)S(1)}, u32[]{:S(2)}, u32[]{:S(2)}) collective-permute-start(f32[6,3,64]{2,0,1:T(8,128)S(1)} %broadcast.740), channel_id=1, source_target_pairs={{4,0},{8,4},{12,8},{16,12},{20,16},{24,20},{28,24},{0,28},{5,1},{9... | collective-permute-start | bytes 13832 | tf_op jit(solution)/shard_map/ppermute | solution.py:34
  13.8 7.1 %collective-permute-start = (f32[24,3,256]{2,0,1:T(8,128)S(1)}, f32[24,3,256]{2,0,1:T(8,128)S(1)}, u32[]{:S(2)}, u32[]{:S(2)}) collective-permute-start(f32[24,3,256]{2,0,1:T(8,128)S(1)} %get-tuple-element.31), channel_id=1, source_target_pairs={{0,4},{4,8},{8,12},{12,16},{16,20},{20,24},{24,28},{28,0},{1,5},{5... | collective-permute-start | bytes 221192 | tf_op jit(solution)/shard_map/ppermute | solution.py:33
  13.9 7.0 %collective-permute-start.1 = (f32[24,3,256]{2,0,1:T(8,128)S(1)}, f32[24,3,256]{2,0,1:T(8,128)S(1)}, u32[]{:S(2)}, u32[]{:S(2)}) collective-permute-start(f32[24,3,256]{2,0,1:T(8,128)S(1)} %get-tuple-element.32), channel_id=1, source_target_pairs={{4,0},{8,4},{12,8},{16,12},{20,16},{24,20},{28,24},{0,28},{5,1},{9... | collective-permute-start | bytes 221192 | tf_op jit(solution)/shard_map/ppermute | solution.py:34
  20.9 18.8 %collective-permute-start.21 = (f32[12,3,128]{2,0,1:T(8,128)S(1)}, f32[12,3,128]{2,0,1:T(8,128)S(1)}, u32[]{:S(2)}, u32[]{:S(2)}) collective-permute-start(f32[12,3,128]{2,0,1:T(8,128)S(1)} %broadcast.703), channel_id=1, source_target_pairs={{4,0},{8,4},{12,8},{16,12},{20,16},{24,20},{28,24},{0,28},{5,1},{9... | collective-permute-start | bytes 55304 | tf_op jit(solution)/shard_map/ppermute | solution.py:34
  30.1 14.3 %collective-permute-start.20 = (f32[12,3,128]{2,0,1:T(8,128)S(1)}, f32[12,3,128]{2,0,1:T(8,128)S(1)}, u32[]{:S(2)}, u32[]{:S(2)}) collective-permute-start(f32[12,3,128]{2,0,1:T(8,128)S(1)} %broadcast.703), channel_id=1, source_target_pairs={{0,4},{4,8},{8,12},{12,16},{16,20},{20,24},{24,28},{28,0},{1,5},{5... | collective-permute-start | bytes 55304 | tf_op jit(solution)/shard_map/ppermute | solution.py:33
  39.6 7.6 %collective-permute-start.4 = (f32[24,3,256]{2,0,1:T(8,128)S(1)}, f32[24,3,256]{2,0,1:T(8,128)S(1)}, u32[]{:S(2)}, u32[]{:S(2)}) collective-permute-start(f32[24,3,256]{2,0,1:T(8,128)S(1)} %get-tuple-element.29), channel_id=1, source_target_pairs={{0,4},{4,8},{8,12},{12,16},{16,20},{20,24},{24,28},{28,0},{1,5},{5... | collective-permute-start | bytes 221192 | tf_op jit(solution)/shard_map/ppermute | solution.py:33
  39.7 8.5 %collective-permute-start.5 = (f32[24,3,256]{2,0,1:T(8,128)S(1)}, f32[24,3,256]{2,0,1:T(8,128)S(1)}, u32[]{:S(2)}, u32[]{:S(2)}) collective-permute-start(f32[24,3,256]{2,0,1:T(8,128)S(1)} %get-tuple-element.30), channel_id=1, source_target_pairs={{4,0},{8,4},{12,8},{16,12},{20,16},{24,20},{28,24},{0,28},{5,1},{9... | collective-permute-start | bytes 221192 | tf_op jit(solution)/shard_map/ppermute | solution.py:34
  60.9 7.9 %collective-permute-start.8 = (f32[24,3,256]{2,0,1:T(8,128)S(1)}, f32[24,3,256]{2,0,1:T(8,128)S(1)}, u32[]{:S(2)}, u32[]{:S(2)}) collective-permute-start(f32[24,3,256]{2,0,1:T(8,128)S(1)} %get-tuple-element.27), channel_id=1, source_target_pairs={{0,4},{4,8},{8,12},{12,16},{16,20},{20,24},{24,28},{28,0},{1,5},{5... | collective-permute-start | bytes 221192 | tf_op jit(solution)/shard_map/ppermute | solution.py:33
  61.0 7.8 %collective-permute-start.9 = (f32[24,3,256]{2,0,1:T(8,128)S(1)}, f32[24,3,256]{2,0,1:T(8,128)S(1)}, u32[]{:S(2)}, u32[]{:S(2)}) collective-permute-start(f32[24,3,256]{2,0,1:T(8,128)S(1)} %get-tuple-element.28), channel_id=1, source_target_pairs={{4,0},{8,4},{12,8},{16,12},{20,16},{24,20},{28,24},{0,28},{5,1},{9... | collective-permute-start | bytes 221192 | tf_op jit(solution)/shard_map/ppermute | solution.py:34
  81.9 7.6 %collective-permute-start.12 = (f32[24,3,256]{2,0,1:T(8,128)S(1)}, f32[24,3,256]{2,0,1:T(8,128)S(1)}, u32[]{:S(2)}, u32[]{:S(2)}) collective-permute-start(f32[24,3,256]{2,0,1:T(8,128)S(1)} %get-tuple-element.25), channel_id=1, source_target_pairs={{0,4},{4,8},{8,12},{12,16},{16,20},{20,24},{24,28},{28,0},{1,5},{5... | collective-permute-start | bytes 221192 | tf_op jit(solution)/shard_map/ppermute | solution.py:33
  81.9 7.5 %collective-permute-start.13 = (f32[24,3,256]{2,0,1:T(8,128)S(1)}, f32[24,3,256]{2,0,1:T(8,128)S(1)}, u32[]{:S(2)}, u32[]{:S(2)}) collective-permute-start(f32[24,3,256]{2,0,1:T(8,128)S(1)} %get-tuple-element.26), channel_id=1, source_target_pairs={{4,0},{8,4},{12,8},{16,12},{20,16},{24,20},{28,24},{0,28},{5,1},{9... | collective-permute-start | bytes 221192 | tf_op jit(solution)/shard_map/ppermute | solution.py:34
  114.6 7.4 %collective-permute-start.25 = (f32[12,3,128]{2,0,1:T(8,128)S(1)}, f32[12,3,128]{2,0,1:T(8,128)S(1)}, u32[]{:S(2)}, u32[]{:S(2)}) collective-permute-start(f32[12,3,128]{2,0,1:T(8,128)S(1)} %get-tuple-element.70), channel_id=1, source_target_pairs={{4,0},{8,4},{12,8},{16,12},{20,16},{24,20},{28,24},{0,28},{5,1},{9... | collective-permute-start | bytes 55304 | tf_op jit(solution)/shard_map/ppermute | solution.py:34
  335.2 6.8 %collective-permute-start.104 = (f32[12,3,128]{2,0,1:T(8,128)S(1)}, f32[12,3,128]{2,0,1:T(8,128)S(1)}, u32[]{:S(2)}, u32[]{:S(2)}) collective-permute-start(f32[12,3,128]{2,0,1:T(8,128)S(1)} %get-tuple-element.61), channel_id=1, source_target_pairs={{0,4},{4,8},{8,12},{12,16},{16,20},{20,24},{24,28},{28,0},{1,5},{5... | collective-permute-start | bytes 55304 | tf_op jit(solution)/shard_map/ppermute | solution.py:33
  335.3 6.7 %collective-permute-start.105 = (f32[12,3,128]{2,0,1:T(8,128)S(1)}, f32[12,3,128]{2,0,1:T(8,128)S(1)}, u32[]{:S(2)}, u32[]{:S(2)}) collective-permute-start(f32[12,3,128]{2,0,1:T(8,128)S(1)} %get-tuple-element.62), channel_id=1, source_target_pairs={{4,0},{8,4},{12,8},{16,12},{20,16},{24,20},{28,24},{0,28},{5,1},{9... | collective-permute-start | bytes 55304 | tf_op jit(solution)/shard_map/ppermute | solution.py:34
  348.4 6.8 %collective-permute-start.108 = (f32[12,3,128]{2,0,1:T(8,128)S(1)}, f32[12,3,128]{2,0,1:T(8,128)S(1)}, u32[]{:S(2)}, u32[]{:S(2)}) collective-permute-start(f32[12,3,128]{2,0,1:T(8,128)S(1)} %get-tuple-element.59), channel_id=1, source_target_pairs={{0,4},{4,8},{8,12},{12,16},{16,20},{20,24},{24,28},{28,0},{1,5},{5... | collective-permute-start | bytes 55304 | tf_op jit(solution)/shard_map/ppermute | solution.py:33
  348.5 6.7 %collective-permute-start.109 = (f32[12,3,128]{2,0,1:T(8,128)S(1)}, f32[12,3,128]{2,0,1:T(8,128)S(1)}, u32[]{:S(2)}, u32[]{:S(2)}) collective-permute-start(f32[12,3,128]{2,0,1:T(8,128)S(1)} %get-tuple-element.60), channel_id=1, source_target_pairs={{4,0},{8,4},{12,8},{16,12},{20,16},{24,20},{28,24},{0,28},{5,1},{9... | collective-permute-start | bytes 55304 | tf_op jit(solution)/shard_map/ppermute | solution.py:34
  386.1 7.7 %collective-permute-start.120 = (f32[24,3,256]{2,0,1:T(8,128)S(1)}, f32[24,3,256]{2,0,1:T(8,128)S(1)}, u32[]{:S(2)}, u32[]{:S(2)}) collective-permute-start(f32[24,3,256]{2,0,1:T(8,128)S(1)} %get-tuple-element.23), channel_id=1, source_target_pairs={{0,4},{4,8},{8,12},{12,16},{16,20},{20,24},{24,28},{28,0},{1,5},{5... | collective-permute-start | bytes 221192 | tf_op jit(solution)/shard_map/ppermute | solution.py:33
  386.1 7.7 %collective-permute-start.121 = (f32[24,3,256]{2,0,1:T(8,128)S(1)}, f32[24,3,256]{2,0,1:T(8,128)S(1)}, u32[]{:S(2)}, u32[]{:S(2)}) collective-permute-start(f32[24,3,256]{2,0,1:T(8,128)S(1)} %get-tuple-element.24), channel_id=1, source_target_pairs={{4,0},{8,4},{12,8},{16,12},{20,16},{24,20},{28,24},{0,28},{5,1},{9... | collective-permute-start | bytes 221192 | tf_op jit(solution)/shard_map/ppermute | solution.py:34
  407.3 7.2 %collective-permute-start.124 = (f32[24,3,256]{2,0,1:T(8,128)S(1)}, f32[24,3,256]{2,0,1:T(8,128)S(1)}, u32[]{:S(2)}, u32[]{:S(2)}) collective-permute-start(f32[24,3,256]{2,0,1:T(8,128)S(1)} %get-tuple-element.21), channel_id=1, source_target_pairs={{0,4},{4,8},{8,12},{12,16},{16,20},{20,24},{24,28},{28,0},{1,5},{5... | collective-permute-start | bytes 221192 | tf_op jit(solution)/shard_map/ppermute | solution.py:33
  407.4 7.1 %collective-permute-start.125 = (f32[24,3,256]{2,0,1:T(8,128)S(1)}, f32[24,3,256]{2,0,1:T(8,128)S(1)}, u32[]{:S(2)}, u32[]{:S(2)}) collective-permute-start(f32[24,3,256]{2,0,1:T(8,128)S(1)} %get-tuple-element.22), channel_id=1, source_target_pairs={{4,0},{8,4},{12,8},{16,12},{20,16},{24,20},{28,24},{0,28},{5,1},{9... | collective-permute-start | bytes 221192 | tf_op jit(solution)/shard_map/ppermute | solution.py:34
  427.8 7.5 %collective-permute-start.128 = (f32[24,3,256]{2,0,1:T(8,128)S(1)}, f32[24,3,256]{2,0,1:T(8,128)S(1)}, u32[]{:S(2)}, u32[]{:S(2)}) collective-permute-start(f32[24,3,256]{2,0,1:T(8,128)S(1)} %get-tuple-element.19), channel_id=1, source_target_pairs={{0,4},{4,8},{8,12},{12,16},{16,20},{20,24},{24,28},{28,0},{1,5},{5... | collective-permute-start | bytes 221192 | tf_op jit(solution)/shard_map/ppermute | solution.py:33
  427.8 7.5 %collective-permute-start.129 = (f32[24,3,256]{2,0,1:T(8,128)S(1)}, f32[24,3,256]{2,0,1:T(8,128)S(1)}, u32[]{:S(2)}, u32[]{:S(2)}) collective-permute-start(f32[24,3,256]{2,0,1:T(8,128)S(1)} %get-tuple-element.20), channel_id=1, source_target_pairs={{4,0},{8,4},{12,8},{16,12},{20,16},{24,20},{28,24},{0,28},{5,1},{9... | collective-permute-start | bytes 221192 | tf_op jit(solution)/shard_map/ppermute | solution.py:34
  (111 other events, 491.0 us)
where the time goes:
time: 459 us; the launch traced here: 450 us
  starting transfers between devices  201 us (44%)
  waiting for transfers between devices  128 us (28%)
  matrix products  101 us (22%)
  local copies, waits for them, and re-layouts  11.7 us (3%)
  other arithmetic  5 us (1%)
    ppermute x66, starting transfers between devices, padded(): after = lax.ppermute(leading, axis, down)  186 us
    ppermute x66, waiting for transfers between devices, padded(): before = lax.ppermute(last, axis, up)  114 us
    dot_general x60, matrix products, along_last(): return jnp.einsum('uvw,jw->uvj', values, matrix, precision=HIGHEST)  39.6 us
    dot_general x87, matrix products, along_middle(): return jnp.einsum('ij,ujw->uiw', matrix, values, precision=HIGHEST)  35.9 us
    dot_general x60, matrix products, along_first(): jnp.dot(matrix, values.reshape(old_shape[0], old_shape[1] * old_shape[2])...  25.7 us
    ppermute x66, starting transfers between devices, padded(): before = lax.ppermute(last, axis, up)  15 us
    ppermute x66, waiting for transfers between devices, padded(): after = lax.ppermute(leading, axis, down)  14.1 us
  transfers between devices with their start and end apart: 132, of which 76 were waited for; matrix products, arithmetic and copies ran while one was open for 12% of the time, Pallas kernels for 0%

commit v1 on v0

v1 whole, which is shorter than its diff:
```python
import functools

import jax
import jax.numpy as jnp
import numpy as np
from jax import lax
from jax.experimental import pallas as pl
from jax.experimental.pallas import tpu as pltpu
from jax.sharding import PartitionSpec as P

TILE = 128
SWEEPS = 3
LEVELS = 4
MASS = tuple(v / 5040 for v in (1, 120, 1191, 2416, 1191, 120, 1))
STIFF = tuple(v / 120 for v in (-1, -24, -15, 80, -15, -24, -1))
SUBDIV = (0.125, 0.5, 0.75, 0.5, 0.125)
OMEGA = 0.5
MESH = pl.DeviceIdType.MESH
WAYS = ((0, 1), (0, -1), (1, 0), (1, 1), (1, -1), (-1, 0), (-1, 1), (-1, -1))


def up8(n):
    return -(-n // 8) * 8


def band(n, size, coeffs):
    i, j = np.indices((size, size))
    out = np.zeros((size, size), np.float32)
    for k, c in enumerate(coeffs):
        out[(j - i + 3 == k) & (i < n) & (j < n)] = c
    return out


def subdivision(n, rows, columns):
    i, j = np.indices((rows, columns))
    out = np.zeros((rows, columns), np.float32)
    for k, c in enumerate(SUBDIV):
        out[(i - 2 * j + 2 == k) & (i < 2 * n) & (j < n)] = c
    return out


def weights(width):
    bands, moves = [], []
    for level in range(LEVELS):
        n = width >> level
        size = max(n, 128)
        mass = band(n, size, (1, 120, 1191, 2416, 1191, 120, 1))
        high = mass.astype(jnp.bfloat16)
        low = (mass - high.astype(np.float32)).astype(jnp.bfloat16)
        stiff = band(n, size, (-1, -24, -15, 80, -15, -24, -1)).astype(jnp.bfloat16)
        bands.append(np.stack([high, low, stiff]))
        if level + 1 < LEVELS:
            move = subdivision(n // 2, size, max(n // 2, 128))
            moves.append((move.astype(jnp.bfloat16), np.ascontiguousarray(move.T).astype(jnp.bfloat16)))
    return bands, moves


def parts(x):
    high = x.astype(jnp.bfloat16)
    return high, (x - high.astype(jnp.float32)).astype(jnp.bfloat16)


def mul(a, b):
    return jnp.dot(a, b, preferred_element_type=jnp.float32)


def taps(x, coeffs):
    sums = (x[0] + x[6], x[1] + x[5], x[2] + x[4], x[3])
    total = coeffs[3] * sums[3]
    for k in range(3):
        total = total + coeffs[k] * sums[k]
    return total


def kernel(sets, n_dir, n_patch, rs, guess, s0, s1, *refs):
    bands, refs = refs[:LEVELS], refs[LEVELS:]
    moves, refs = refs[: 2 * (LEVELS - 1)], refs[2 * (LEVELS - 1) :]
    out, refs = refs[0], refs[1:]
    bufs = []
    for _ in sets:
        bufs.append(refs[:6])
        refs = refs[6:]
    fields = []
    for level in range(LEVELS):
        fields.append(refs[:6])
        refs = refs[6:]
    send_sem, recv_sem = refs
    masks = (s0, s1, None, None)

    me_u, me_v = lax.axis_index("dir"), lax.axis_index("patch")
    has_down, has_up = me_u > 0, me_u < n_dir - 1

    def device(a, b):
        return {"dir": me_u + a, "patch": lax.rem(me_v + b + n_patch, n_patch)}

    def when_way(a, body):
        if a == 0:
            body()
        else:
            pl.when(has_up if a > 0 else has_down)(body)

    barrier = pltpu.get_barrier_semaphore()
    for step in (0, 1, -1):
        def greet():
            for a, b in WAYS:
                if a == step:
                    pl.semaphore_signal(barrier, inc=1, device_id=device(a, b), device_id_type=MESH)
        when_way(step, greet)

    for (nu, nv, nvp, w), (c, sl, sr, rl, rr, p) in zip(sets, bufs):
        p[:, nvp + 8 :, :] = jnp.zeros((nu + 6, 8, w), jnp.float32)
        for flag, at in ((me_u == 0, 0), (me_u == n_dir - 1, nu + 3)):
            @pl.when(flag)
            def _():
                c[:, at : at + 3] = jnp.zeros((2, 3, nvp, w), jnp.float32)
                rl[:, at : at + 3] = jnp.zeros((2, 3, 3, w), jnp.float32)
                rr[:, at : at + 3] = jnp.zeros((2, 3, 3, w), jnp.float32)

    inside = jnp.logical_and(has_down, has_up)
    pl.when(inside)(lambda: pl.semaphore_wait(barrier, 8))
    pl.when(jnp.logical_not(inside))(lambda: pl.semaphore_wait(barrier, 5))

    def exchange(which, x, number):
        nu, nv, nvp, w = sets[which]
        c, sl, sr, rl, rr, p = bufs[which]
        slot = lax.rem(number, 2)

        def stage(u, _):
            row = x[u]
            c[slot, u + 3] = row
            sl[slot, u] = row[0:3]
            sr[slot, u] = row[nv - 3 : nv]
            return 0

        lax.fori_loop(0, nu, stage, 0, unroll=min(nu, 4))

        def copy(index):
            a, b = WAYS[index]
            if b == 0:
                at, to = (nu, 0) if a > 0 else (3, nu + 3)
                src, dst = c.at[slot, at : at + 3], c.at[slot, to : to + 3]
            else:
                near, far = (sr, rl) if b > 0 else (sl, rr)
                if a == 0:
                    src, dst = near.at[slot], far.at[slot, 3 : nu + 3]
                else:
                    at, to = (nu - 3, 0) if a > 0 else (0, nu + 3)
                    src, dst = near.at[slot, at : at + 3], far.at[slot, to : to + 3]
            return pltpu.make_async_remote_copy(
                src_ref=src,
                dst_ref=dst,
                send_sem=send_sem.at[slot, index],
                recv_sem=recv_sem.at[slot, index],
                device_id=device(a, b),
                device_id_type=MESH,
            )

        for step in (1, -1, 0):
            def start():
                for index, (a, b) in enumerate(WAYS):
                    if a == step:
                        copy(index).start()
            when_way(step, start)
        for step in (0, 1, -1):
            def finish():
                for index, (a, b) in enumerate(WAYS):
                    if a == step:
                        copy(index).wait_send()
                    if a == -step:
                        copy(index).wait_recv()
            when_way(step, finish)

        def gather(u, _):
            p[u, 8 : 8 + nvp] = c[slot, u]
            p[u, 5:8] = rl[slot, u]
            p[u, 8 + nv : 11 + nv] = rr[slot, u]
            return 0

        lax.fori_loop(0, nu + 6, gather, 0, unroll=3)

    def chunked(which, body):
        nu, nv, nvp, w = sets[which]
        size = nu
        while size * nvp > 192 and size % 2 == 0:
            size //= 2
        if size == nu:
            body(0, nu)
        else:
            lax.fori_loop(0, nu // size, lambda i, _: (body(i * size, size), 0)[1], 0)

    def operate(level, x, number, use):
        which = set_of[level]
        nu, nv, nvp, w = sets[which]
        p = bufs[which][5]
        load, field, pu, ku, g, h = fields[level]
        exchange(which, x, number)

        def sublanes(u, _):
            t = [p[u, 5 + k : 5 + k + nvp, :] for k in range(7)]
            pu[u] = taps(t, [v / 5040 for v in MASS])
            ku[u] = taps(t, [v / 5040 for v in STIFF])
            return 0

        lax.fori_loop(0, nu + 6, sublanes, 0, unroll=2)

        def leading(u, _):
            a = [pu[u + k] for k in range(7)]
            b = [ku[u + k] for k in range(7)]
            g[u] = taps(a, STIFF) + taps(b, MASS)
            h[u] = taps(a, [v * 42 for v in MASS])
            return 0

        lax.fori_loop(0, nu, leading, 0, unroll=2)
        table = bands[level]

        def finish(u, size):
            g_high, g_low = parts(g[pl.ds(u, size)].reshape(size * nvp, w))
            h_high, h_low = parts(h[pl.ds(u, size)].reshape(size * nvp, w))
            value = mul(g_high, table[0]) + mul(g_low, table[0]) + mul(g_high, table[1])
            value = value + mul(h_high, table[2]) + mul(h_low, table[2])
            use(pl.ds(u, size), value.reshape(size, nvp, w))

        chunked(which, finish)

    def sweep(level, number):
        load, field = fields[level][:2]
        mask = masks[level]

        def use(at, value):
            update = (OMEGA / 2**level) * load[at] - OMEGA * value
            if mask is not None:
                update = update * mask[at]
            field[at] = field[at] + update

        operate(level, field, number, use)

    def sweeps(level, count, number):
        def body(i, _):
            sweep(level, number + i)
            return 0

        lax.fori_loop(0, count, body, 0)
        return number + count

    def descend(level, number):
        which = set_of[level]
        nu, nv, nvp, w = sets[which]
        load, field, pu, ku, g, h = fields[level]
        mask = masks[level]
        if level == 0:
            number = sweeps(level, SWEEPS, number)
        else:
            first = (OMEGA / 2**level) * load[...]
            field[...] = first if mask is None else first * mask[...]
            number = sweeps(level, SWEEPS - 1, number)
        if level + 1 < LEVELS:
            low_which = 1 if level == 0 else which
            low_p = bufs[low_which][5]
            down, up = moves[2 * level], moves[2 * level + 1]
            lanes = down.shape[1]

            def residual(at, value):
                r = load[at] - float(2**level) * value
                if mask is not None:
                    r = r * mask[at]
                size = r.shape[0]
                r_high, r_low = parts(r.reshape(size * nvp, w))
                n = mul(r_high, down[...]) + mul(r_low, down[...])
                g[at, :, 0:lanes] = n.reshape(size, nvp, lanes)

            operate(level, field, number, residual)
            number += 1
            exchange(low_which, g.at[:, :, 0:lanes], number)
            number += 1
            cu, cv, cvp, cw = sets[set_of[level + 1]]
            c_load, c_field = fields[level + 1][:2]
            c_p = bufs[set_of[level + 1]][5]
            c_load[...] = jnp.zeros((cu, cvp, cw), jnp.float32)
            for i in range(cu):
                total = None
                for k in range(5):
                    line = None
                    for m in range(5):
                        term = SUBDIV[m] * low_p[2 * i + k + 1, pl.ds(6 + m, cv, stride=2), :]
                        line = term if line is None else line + term
                    total = SUBDIV[k] * line if total is None else total + SUBDIV[k] * line
                c_load[i, 0:cv, :] = total
            number = descend(level + 1, number)
            exchange(set_of[level + 1], c_field, number)
            number += 1
            for u in range(nu):
                i = u // 2 + 3
                mix = ((i - 1, 0.125), (i, 0.75), (i + 1, 0.125)) if u % 2 == 0 else ((i, 0.5), (i + 1, 0.5))
                shifted = []
                for d in range(3):
                    total = None
                    for row, c in mix:
                        term = c * c_p[row, 7 + d : 7 + d + cv, :]
                        total = term if total is None else total + term
                    shifted.append(total)
                before, here, after = shifted
                spread[level][u, pl.ds(0, cv, stride=2), :] = 0.125 * (before + after) + 0.75 * here
                spread[level][u, pl.ds(1, cv, stride=2), :] = 0.5 * (here + after)

            def correct(at, size):
                at = pl.ds(at, size)
                y_high, y_low = parts(spread[level][at].reshape(size * nvp, lanes))
                y = (mul(y_high, up[...]) + mul(y_low, up[...])).reshape(size, nvp, w)
                if mask is not None:
                    y = y * mask[at]
                field[at] = field[at] + y

            chunked(which, correct)
        return sweeps(level, SWEEPS, number)

    set_of = [0, 2, 3, 4]
    spread = [bufs[1][0].at[0]] + [fields[level][3] for level in range(1, LEVELS)]
    load, field = fields[0][:2]
    load[...] = rs[...]
    field[...] = guess[...] * s0[...]
    descend(0, 0)
    out[...] = field[...]


def on_device(right_side, guess, mask_fine, mask_next):
    nu, nv, nw = right_side.shape
    sets = [(nu, nv, up8(nv), nw), (nu, nv, up8(nv), max(nw // 2, 128))]
    for level in range(1, LEVELS):
        sets.append((nu >> level, nv >> level, up8(nv >> level), max(nw >> level, 128)))
    sets = tuple(sets)
    bands, moves = weights(nw)
    s0 = jnp.repeat(mask_fine.astype(jnp.float32), TILE, axis=2)
    s1 = jnp.repeat(mask_next.astype(jnp.float32), TILE, axis=2)
    s1 = jnp.pad(s1, ((0, 0), (0, sets[2][2] - sets[2][1]), (0, sets[2][3] - s1.shape[2])))
    operands = [right_side, guess, s0, s1] + [jnp.asarray(b) for b in bands]
    operands += [jnp.asarray(m) for pair in moves for m in pair]
    scratch = []
    for u, v, vp, w in sets:
        scratch += [pltpu.VMEM((2, u + 6, vp, w), jnp.float32)]
        scratch += [pltpu.VMEM((2, u, 3, w), jnp.float32)] * 2
        scratch += [pltpu.VMEM((2, u + 6, 3, w), jnp.float32)] * 2
        scratch += [pltpu.VMEM((u + 6, vp + 16, w), jnp.float32)]
    for which in (0, 2, 3, 4):
        u, v, vp, w = sets[which]
        scratch += [pltpu.VMEM((u, vp, w), jnp.float32)] * 2
        scratch += [pltpu.VMEM((u + 6, vp, w), jnp.float32)] * 2
        scratch += [pltpu.VMEM((u, vp, w), jnp.float32)] * 2
    scratch += [pltpu.SemaphoreType.DMA((2, 8)), pltpu.SemaphoreType.DMA((2, 8))]
    vmem = pl.BlockSpec(memory_space=pltpu.VMEM)
    return pl.pallas_call(
        functools.partial(kernel, sets, lax.axis_size("dir"), lax.axis_size("patch")),
        out_shape=jax.ShapeDtypeStruct(right_side.shape, jnp.float32),
        in_specs=[vmem] * len(operands),
        out_specs=vmem,
        scratch_shapes=scratch,
        compiler_params=pltpu.CompilerParams(
            collective_id=0, has_side_effects=True, vmem_limit_bytes=60 * 2**20
        ),
        name="vcycle",
    )(*operands)


def solution(mesh):
    spec = P("dir", "patch", None)
    return jax.shard_map(
        on_device, mesh=mesh, in_specs=(spec,) * 4, out_specs=spec, check_vma=False
    )
```

time: 459 us -> 185 us (0.40); the launches traced: 450 us -> 184 us
  starting transfers between devices: 201 us -> 0 us
  Pallas kernels: 0 us -> 179 us
  waiting for transfers between devices: 128 us -> 0 us
  matrix products: 101 us -> 0 us
  local copies, waits for them, and re-layouts: 11.7 us -> 4.96 us
    ppermute x132 -> x0, starting transfers between devices: 201 us -> none  [the longest x66 186 us: padded(): after = lax.ppermute(leading, axis, down)]
    pallas_call x0 -> x1, Pallas kernels: none -> 179 us  [on_device(): pl.pallas_call(functools.partial(kernel, sets, lax.axis_size('dir'), lax....]
    ppermute x132 -> x0, waiting for transfers between devices: 128 us -> none  [the longest x66 114 us: padded(): before = lax.ppermute(last, axis, up)]
    dot_general x207 -> x0, matrix products: 101 us -> none  [the longest x60 39.6 us: along_last(): return jnp.einsum('uvw,jw->uvj', values, matrix, precision=HIGHEST)]
  transfers between devices with their start and end apart: 132 -> 0, of which waited for: 76 -> 0; matrix products, arithmetic and copies ran while one was open for 12% -> 0% of each run, Pallas kernels for 0% -> 0%
where the time goes in v1:
time: 185 us; the launch traced here: 184 us
  Pallas kernels  179 us (97%)
  local copies, waits for them, and re-layouts  4.96 us (3%)
    pallas_call x1, Pallas kernels, on_device(): pl.pallas_call(functools.partial(kernel, sets, lax.axis_size('dir'), lax....  179 us

profile of v1, /device:TPU:0, one launch (start us, length us, event | category | flops | bytes accessed | tf_op | source)
XLA Modules:
  0.0 184.3 jit_solution(10838075878455153434)
XLA Ops:
  0.0 0.0 copy-start
  0.0 0.7 convert_element_type.11
  0.7 0.0 copy-done
  0.8 0.1 reshape.8
  0.9 0.6 pad.4.s1
  1.5 0.2 copy.15
  1.7 0.8 broadcast_in_dim.4
  2.5 1.3 reshape.7.s0
  3.8 178.6 %vcycle.1 = f32[24,24,256]{2,1,0:T(8,128)} custom-call(f32[24,24,256]{2,1,0:T(8,128)} %rs.1, f32[24,24,256]{2,1,0:T(8,128)} %guess.1, f32[24,24,256]{2,1,0:T(8,128)} %reshape.7.s0, f32[12,16,128]{2,1,0:T(8,128)} %pad.4.s1, bf16[3,256,256]{2,1,0:T(8,128)(2,1)} %constant.23.clone.refs_0_, bf16[3,128,128]{2,1,0:T(8,128)(2,1)} %constant.24.clone.refs_1_, ...), custom_call_target="tpu_custom_call" | custom-call | tf_op jit(solution)/shard_map/vcycle/pallas_call | solution.py:350
  182.3 1.9 %copy.20 = f32[24,24,256]{2,1,0:T(8,128)} copy(f32[24,24,256]{2,1,0:T(8,128)} %vcycle.1) | data formatting | bytes 1179648
  (2 shorter events, 0.0 us)
Async XLA Ops:
  0.0 0.8 copy-start
